TPU v7x, 256 devices: a whole 4x4x8 slice. The times are simulated.
256 devices in a mesh: section: 4 (over x), tok: 32 (over z, y), head: 2 (over core).
Axes of the slice: x: 4, y: 4, z: 8, core: 2. Of those that a mesh axis runs over, the one named last changes fastest.
Arguments:
- group_in: bfloat16 [4, 4096, 2048], P('section', 'tok'), may hold values from -6 to 6
- w_qkv: bfloat16 [4, 3, 2048, 2048], P('section', None, 'tok', 'head'), may hold values from -0.125 to 0.125
- w_out: bfloat16 [4, 2048, 2048], P('section', 'head', 'tok'), may hold values from -0.125 to 0.125
- step_sizes: float32 [4, 4096, 4], P('section', 'tok', 'head'), may hold values from 0.05 to 1
- fast_weights: bfloat16 [4, 4, 3, 512, 512], P('section', 'head'), may hold values from -0.25 to 0.25
- momentum: bfloat16 [4, 4, 3, 512, 512], P('section', 'head'), may hold values from -48 to 48
- momentum_decay: float32 [4, 4], P('section', 'head'), may hold values from 0.5 to 0.95
- fast_rate: float32 [4, 4], P('section', 'head'), may hold values from 0.3 to 1
Outputs:
- handed: bfloat16 [4, 4096, 2048], P('section', 'tok', 'head')
- fast_next: bfloat16 [4, 4, 3, 512, 512], P('section', 'head')
All inputs are finite; a program needn't handle non-finite values.
Results may differ from a plain program's by a relative error of at most 0.015.
Values may be sent and summed in bfloat16 or wider, within the bound.
No kernel may reach another device: no remote copies, remote signals or barrier semaphores. Data moves between devices by JAX's collectives and lax.ppermute only.
A program may use at most 128 MiB of HBM per device.

v0:
```python
import jax
import jax.numpy as jnp
from jax import lax
from jax.sharding import Mesh
from jax.sharding import PartitionSpec as P

NS_ITERS = 2
TOK = ("tok_0", "tok_1")
coef_linear = 3.4445
coef_cubic = -4.775
coef_quintic = 2.0315


def gathered_by_axis(shard, axes, dim):
    if not axes:
        return shard
    nearer = lax.all_gather(shard, axes[-1], axis=dim, tiled=True)
    return gathered_by_axis(nearer, axes[:-1], dim)


def split_up(shard, dim, count):
    lengths = shard.shape
    blocks = shard.reshape(*lengths[:dim], count, lengths[dim] // count, *lengths[dim + 1 :])
    return jnp.moveaxis(blocks, dim, 0)


def sum_at_owner(shard, axis, dim):
    count = lax.axis_size(axis)
    blocks = lax.all_to_all(split_up(shard, dim, count), axis, 0, 0, tiled=True)
    return jnp.sum(blocks.astype(jnp.float32), axis=0)


def passed_along(value, axis, steps):
    count = lax.axis_size(axis)
    pairs = [(source, (source + steps) % count) for source in range(count)]
    return lax.ppermute(value, axis, pairs)


def rms_rows(values_in, epsilon):
    return values_in * lax.rsqrt(jnp.mean(values_in * values_in, axis=-1, keepdims=True) + epsilon)


def fast_grads(key_rows, value_rows, step_rates, weights):
    gate_pre = jnp.einsum(
        "thi,hij->thj", key_rows, weights[:, 0], preferred_element_type=jnp.float32
    )
    up_pre = jnp.einsum("thi,hij->thj", key_rows, weights[:, 1], preferred_element_type=jnp.float32)
    squash = jax.nn.sigmoid(gate_pre)
    hidden = (gate_pre * squash * up_pre).astype(jnp.bfloat16)
    errors = (-(step_rates[:, :, None] * value_rows.astype(jnp.float32))).astype(jnp.bfloat16)
    back_hidden = jnp.einsum(
        "thi,hij->thj", errors, weights[:, 2], preferred_element_type=jnp.float32
    )
    grad_gate = (back_hidden * up_pre * squash * (1.0 + gate_pre * (1.0 - squash))).astype(
        jnp.bfloat16
    )
    grad_up = (back_hidden * gate_pre * squash).astype(jnp.bfloat16)
    grad_first = jnp.einsum("thi,thj->hij", key_rows, grad_gate, preferred_element_type=jnp.float32)
    grad_third = jnp.einsum("thi,thj->hij", key_rows, grad_up, preferred_element_type=jnp.float32)
    grad_second = jnp.einsum("thi,thj->hij", errors, hidden, preferred_element_type=jnp.float32)
    return jnp.stack([grad_first, grad_third, grad_second], axis=1)


def newton_step(rows_in, gathered):
    gram_matrix = jnp.einsum(
        "mij,mik->mjk", gathered, gathered, preferred_element_type=jnp.float32
    ).astype(jnp.bfloat16)
    cubic_term = jnp.einsum(
        "mij,mjk->mik", rows_in, gram_matrix, preferred_element_type=jnp.float32
    )
    quintic_term = jnp.einsum(
        "mij,mjk->mik",
        cubic_term.astype(jnp.bfloat16),
        gram_matrix,
        preferred_element_type=jnp.float32,
    )
    return (
        coef_linear * rows_in.astype(jnp.float32)
        + coef_cubic * cubic_term
        + coef_quintic * quintic_term
    ).astype(jnp.bfloat16)


def apply_fast(queries, updated):
    gate_pre = jnp.einsum(
        "thi,hij->thj", queries, updated[:, 0], preferred_element_type=jnp.float32
    )
    up_pre = jnp.einsum("thi,hij->thj", queries, updated[:, 1], preferred_element_type=jnp.float32)
    hidden = (jax.nn.silu(gate_pre) * up_pre).astype(jnp.bfloat16)
    output = jnp.einsum("thj,hij->thi", hidden, updated[:, 2], preferred_element_type=jnp.float32)
    return rms_rows(output, 1e-05).astype(jnp.bfloat16)


def shards(group_in, w_qkv, w_out, step_sizes, fast_weights, momentum, momentum_decay, fast_rate):
    tokens = group_in[0]
    tok_rows = tokens.shape[0]
    local_heads = fast_weights.shape[1]
    fan_width = fast_weights.shape[3]
    hid_width = fast_weights.shape[4]
    half_width = w_qkv.shape[3]
    projected = jnp.einsum(
        "td,jde->jte",
        tokens,
        lax.all_gather(w_qkv[0], TOK, axis=1, tiled=True),
        preferred_element_type=jnp.float32,
    )
    shaped = projected.reshape(3, tok_rows, local_heads, fan_width)
    queries = rms_rows(shaped[0], 1e-06).astype(jnp.bfloat16)
    key_rows = rms_rows(shaped[1], 1e-06).astype(jnp.bfloat16)
    value_rows = shaped[2].astype(jnp.bfloat16)
    gradients = fast_grads(key_rows, value_rows, step_sizes[0], fast_weights[0])
    decay_rate = momentum_decay[0][:, None, None, None]
    summed = lax.psum(gradients.astype(jnp.bfloat16), TOK).astype(jnp.float32)
    moment = decay_rate * momentum[0].astype(jnp.float32) + summed
    norm_values = jnp.sqrt(jnp.sum(moment * moment, axis=(2, 3), keepdims=True))
    iterate = (moment / (norm_values + 1e-06)).astype(jnp.bfloat16)
    iterate = iterate.reshape(local_heads * 3, fan_width, hid_width)
    for number in range(NS_ITERS):
        iterate = newton_step(iterate, iterate)
    iterate = iterate.reshape(local_heads, 3, fan_width, hid_width)
    updated = (
        fast_weights[0].astype(jnp.float32)
        - fast_rate[0][:, None, None, None] * iterate.astype(jnp.float32)
    ).astype(jnp.bfloat16)
    mixed_heads = apply_fast(queries, updated).reshape(tok_rows, half_width)
    partial_out = jnp.dot(
        mixed_heads, gathered_by_axis(w_out[0], TOK, 1), preferred_element_type=jnp.float32
    )
    summed_out = sum_at_owner(partial_out.astype(jnp.bfloat16), "head", 1)
    share_width = summed_out.shape[1]
    own_tokens = lax.dynamic_slice_in_dim(
        tokens, lax.axis_index("head") * share_width, share_width, 1
    )
    layer_out = (own_tokens.astype(jnp.float32) + summed_out).astype(jnp.bfloat16)
    handed = passed_along(layer_out[None], "section", 1)
    return (handed, updated[None])


def solution(mesh):
    torus = Mesh(
        mesh.devices.reshape(mesh.shape["section"], 8, 4, mesh.shape["head"]),
        ("section", "tok_0", "tok_1", "head"),
    )
    return jax.shard_map(
        shards,
        mesh=torus,
        in_specs=(
            P("section", TOK, None),
            P("section", None, TOK, "head"),
            P("section", "head", TOK),
            P("section", TOK, "head"),
            P("section", "head", None, None, None),
            P("section", "head", None, None, None),
            P("section", "head"),
            P("section", "head"),
        ),
        out_specs=(P("section", TOK, "head"), P("section", "head", None, None, None)),
        check_vma=False,
    )
```

profile of v0, /device:TPU:1, one launch (start us, length us, event | category | flops | bytes accessed | tf_op | source)
XLA Modules:
  0.0 375.4 jit_solution(4437180911537350289)
XLA Ops:
  8.0 0.0 all-gather.6.cloned.1.call-start
  8.0 0.7 all-gather.6.cloned.1.call-update
  8.7 0.0 all-reduce.2.cloned.1.call-start
  8.8 2.1 copy.71
  10.9 122.4 %all-gather.6.cloned.1.call-done = bf16[1,3,2048,1024]{3,2,1,0:T(8,128)(2,1)} async-done(((bf16[1,3,64,1024]{3,2,1,0:T(8,128)(2,1)}), bf16[1,3,2048,1024]{3,2,1,0:T(8,128)(2,1)}) %all-gather.6.cloned.1.call-update) | async-done | bytes 12582928 | tf_op jit(solution)/shard_map/all_gather | solution.py:104
  133.3 6.6 %fusion.19 = f32[3,128,1024]{1,2,0:T(8,128)S(1)} fusion(bf16[1,3,2048,1024]{3,2,1,0:T(8,128)(2,1)} %all-gather.6.cloned.1.call-done, bf16[1,128,2048]{2,1,0:T(8,128)(2,1)} %param.8), kind=kOutput, calls=%fused_computation.27 | convolution fusion | flops 1610612736 | bytes 14680064 | tf_op jit(solution)/shard_map/td,jde->jte/dot_general | solution.py:101
  139.9 0.9 fusion.46
  140.8 0.1 multiply_reduce_fusion.3
  140.9 0.3 convolution_bitcast_fusion.3
  141.3 0.3 convolution_bitcast_fusion.4
  141.6 0.0 copy-done.10
  141.7 0.3 convolution_bitcast_fusion.5
  142.0 0.5 fusion.23
  142.5 0.5 fusion.22
  143.0 0.5 fusion.24
  143.5 0.0 copy-start.6
  143.5 2.0 pad_maximum_fusion
  145.5 0.0 all-reduce.2.cloned.1.call-update
  145.6 0.0 all-gather.8.cloned.1.call-start
  145.6 0.0 copy-done.6
  145.6 10.9 %all-gather.1 = bf16[1,1024,256]{1,2,0:T(8,128)(2,1)} all-gather(bf16[1,1024,64]{1,2,0:T(8,128)(2,1)S(1)} %copy-done.6), channel_id=3, replica_groups=mesh['section'=4,'tok_0'=8,'tok_1'=4,'head'=2] {'tok_1'}, dimensions={2}, use_global_device_ids=true | all-gather | bytes 655360 | tf_op jit(solution)/shard_map/all_gather | solution.py:17
  156.6 0.0 all-gather.8.cloned.1.call-update
  156.6 1.1 multiply_reduce_fusion.2
  157.7 2.0 copy.44
  159.8 157.7 %all-reduce.2.cloned.1.call-done = bf16[2,3,512,512]{3,2,0,1:T(8,128)(2,1)} async-done(((bf16[2,3,512,512]{3,2,0,1:T(8,128)(2,1)}), bf16[2,3,512,512]{3,2,0,1:T(8,128)(2,1)}) %all-reduce.2.cloned.1.call-update) | async-done | bytes 3145744 | tf_op jit(solution)/shard_map/psum | solution.py:113
  317.5 0.0 copy-done.2
  317.5 0.0 copy-done.9
  317.5 3.5 multiply_reduce_fusion
  321.0 0.0 copy-done.3
  321.0 1.3 divide_convert_fusion
  322.3 0.2 copy.40
  322.5 1.8 convolution_convert_fusion.1
  324.3 1.8 fusion.47
  326.1 2.2 add_convert_fusion.1
  328.4 1.8 convolution_convert_fusion
  330.2 1.8 fusion.48
  332.0 0.0 copy-start.8
  332.0 2.5 fusion.7
  334.5 0.0 copy-start
  334.5 0.0 copy-done.8
  334.6 0.0 copy-start.5
  334.6 5.4 %fusion.4 = bf16[2,3,512,512]{3,2,0,1:T(8,128)(2,1)S(1)} fusion(f32[2,3,512,512]{3,2,1,0:T(8,128)S(1)} %bitcast.115, f32[2]{0:T(128)S(1)} %bitcast.131, bf16[1,2,3,512,512]{4,3,2,1,0:T(8,128)(2,1)} %param.12), kind=kLoop, calls=%fused_computation.6 | loop fusion | flops 6291456 | bytes 12582920 | tf_op jit(solution)/shard_map/convert_element_type | solution.py:124
  339.9 0.0 copy-done
  339.9 0.0 copy-start.4
  340.0 1.7 copy-done.4
  341.6 0.0 copy-done.5
  341.6 1.1 convolution_bitcast_fusion.1
  342.7 2.6 multiply_reduce_fusion.1
  345.3 0.1 multiply_convert_fusion
  345.4 0.0 all-gather.8.cloned.1.call-done
  345.4 0.0 copy-start.7
  345.4 0.0 slice-start.1
  345.5 3.9 %fusion.16 = bf16[128,2048]{1,0:T(8,128)(2,1)S(1)} fusion(bf16[128,1024]{0,1:T(8,128)(2,1)S(1)} %bitcast.130, bf16[1,1024,2048]{1,2,0:T(8,128)(2,1)} %all-gather.8.cloned.1.call-done), kind=kOutput, calls=%fused_computation.21 | convolution fusion | flops 537133056 | bytes 4980736 | tf_op jit(solution)/shard_map/dot_general | solution.py:126
  349.3 0.0 copy-start.1
  349.4 8.9 %all_to_all.5 = bf16[2,128,1024]{2,1,0:T(8,128)(2,1)S(1)} all-to-all(bf16[2,128,1024]{2,1,0:T(8,128)(2,1)S(1)} %bitcast.127), channel_id=1, replica_groups=mesh['section'=4,'tok_0'=8,'tok_1'=4,'head'=2] {'head'}, dimensions={0} | all-to-all | bytes 1048576 | tf_op jit(solution)/shard_map/all_to_all | solution.py:29
  358.3 0.1 convert_reduce_fusion
  358.4 0.0 copy-done.7
  358.4 0.1 fusion.29
  358.4 1.3 collective-permute-start
  359.7 0.0 slice-done
  359.7 0.0 slice-done.1
  359.7 2.8 subtract_convert_fusion
  362.5 4.7 %collective-permute-done = bf16[1,128,1024]{2,1,0:T(8,128)(2,1)S(1)} collective-permute-done((bf16[1,128,1024]{2,1,0:T(8,128)(2,1)S(1)}, bf16[1,128,1024]{2,1,0:T(8,128)(2,1)S(1)}, u32[]{:S(2)}, u32[]{:S(2)}) %collective-permute-start) | collective-permute-done | bytes 262176 | tf_op jit(solution)/shard_map/ppermute | solution.py:36
  367.2 0.7 copy.75
  (14 shorter events, 0.2 us)
Async XLA Ops:
  8.0 125.3 %all-gather.6.cloned.1.call-start = ((), (), s32[]{:S(2)}) async-start(), calls=%async_computation.2 | async-start | bytes 12976128 | tf_op jit(solution)/shard_map/all_gather | solution.py:104
  8.7 308.8 %all-reduce.2.cloned.1.call-start = ((), (), s32[]{:S(2)}) async-start(), calls=%async_computation.1 | async-start | bytes 6291456 | tf_op jit(solution)/shard_map/psum | solution.py:113
  140.8 0.9 copy-start.10
  143.5 2.1 copy-start.6
  145.5 172.0 %copy-start.2 = (bf16[1,2,3,512,512]{4,3,2,1,0:T(8,128)(2,1)S(1)}, bf16[1,2,3,512,512]{4,3,2,1,0:T(8,128)(2,1)}, u32[]{:S(2)}) copy-start(bf16[1,2,3,512,512]{4,3,2,1,0:T(8,128)(2,1)} %param.13) | copy-start | bytes 9437188
  145.5 172.0 %copy-start.9 = (f32[1,2]{1,0:T(1,128)S(1)}, f32[1,2]{1,0:T(1,128)}, u32[]{:S(2)}) copy-start(f32[1,2]{1,0:T(1,128)} %param.14) | copy-start | bytes 28
  145.6 199.9 %all-gather.8.cloned.1.call-start = ((), (), s32[]{:S(2)}) async-start(), calls=%async_computation.3 | async-start | bytes 4718592 | tf_op jit(solution)/shard_map/all_gather | solution.py:17
  317.5 3.5 copy-start.3
  332.0 2.5 copy-start.8
  334.5 5.4 %copy-start = (f32[6,512,512]{2,1,0:T(8,128)}, f32[6,512,512]{2,1,0:T(8,128)S(1)}, u32[]{:S(2)}) copy-start(f32[6,512,512]{2,1,0:T(8,128)S(1)} %fusion.7) | copy-start | bytes 18874372
  334.6 7.1 %copy-start.5 = (f32[128,2,512]{2,0,1:T(8,128)S(1)}, f32[128,2,512]{2,0,1:T(8,128)}, u32[]{:S(2)}) copy-start(f32[128,2,512]{2,0,1:T(8,128)} %copy.44) | copy-start | bytes 1572868
  339.9 1.7 copy-start.4
  342.7 17.0 %slice-start = ((s8[6291456]{0:T(1024)(128)(4,1)}), s8[2097152]{0:T(1024)(128)(4,1)S(1)}, s32[]{:S(2)}) async-start(s8[6291456]{0:T(1024)(128)(4,1)} %bitcast.116), calls=%async_computation.4 | async-start | bytes 4194304
  345.4 12.9 %copy-start.7 = (bf16[1,128,2048]{2,1,0:T(8,128)(2,1)S(1)}, bf16[1,128,2048]{2,1,0:T(8,128)(2,1)}, u32[]{:S(2)}) copy-start(bf16[1,128,2048]{2,1,0:T(8,128)(2,1)} %param.8) | copy-start | bytes 1572868
  345.4 14.3 %slice-start.1 = ((s8[6291456]{0:T(1024)(128)(4,1)}), s8[4194304]{0:T(1024)(128)(4,1)S(1)}, s32[]{:S(2)}) async-start(s8[6291456]{0:T(1024)(128)(4,1)} %bitcast.116), calls=%async_computation.5 | async-start | bytes 8388608
  349.3 10.4 %copy-start.1 = (bf16[1,2,3,512,512]{4,3,2,1,0:T(8,128)(2,1)S(1)}, bf16[1,2,3,512,512]{4,3,2,1,0:T(8,128)(2,1)}, u32[]{:S(2)}) copy-start(bf16[1,2,3,512,512]{4,3,2,1,0:T(8,128)(2,1)} %param.12) | copy-start | bytes 9437188
  358.4 8.8 %collective-permute-start = (bf16[1,128,1024]{2,1,0:T(8,128)(2,1)S(1)}, bf16[1,128,1024]{2,1,0:T(8,128)(2,1)S(1)}, u32[]{:S(2)}, u32[]{:S(2)}) collective-permute-start(bf16[1,128,1024]{2,1,0:T(8,128)(2,1)S(1)} %fusion.29), channel_id=1, source_target_pairs={{0,64},{64,128},{128,192},{192,0},{1,65},{65,129},{129,193},{193,1... | collective-permute-start | bytes 786440 | tf_op jit(solution)/shard_map/ppermute | solution.py:36
Sparse Core Ops, SparseCore 0:
  11.4 121.8 all-gather.5
  145.7 171.7 all-reduce.1
Sparse Core Ops, SparseCore 1:
  156.7 64.3 all-gather.7
where the time goes:
time: 376 us; the launch traced here: 375 us
  waiting for transfers between devices  286 us (76%)
  matrix products  28.7 us (8%)
  blocking collectives  19.8 us (5%)
  other arithmetic  16.4 us (4%)
  between operations  15.8 us (4%)
  local copies, waits for them, and re-layouts  7.67 us (2%)
    psum x1, waiting for transfers between devices, shards(): summed = lax.psum(gradients.astype(jnp.bfloat16), TOK).astype(jnp.float32)  158 us
    all_gather x1, waiting for transfers between devices, shards(): lax.all_gather(w_qkv[0], TOK, axis=1, tiled=True)  122 us
    all_gather x1, blocking collectives, gathered_by_axis(): nearer = lax.all_gather(shard, axes[-1], axis=dim, tiled=True)  10.9 us
    all_to_all x1, blocking collectives, sum_at_owner(): blocks = lax.all_to_all(split_up(shard, dim, count), axis, 0, 0, tiled=True)  8.89 us
    convert_element_type x2, other arithmetic, shards(): updated = (fast_weights[0].astype(jnp.float32) - fast_rate[0][:, None, No...  8.16 us
  transfers between devices with their start and end apart: 4, of which 3 were waited for; matrix products, arithmetic and copies ran while one was open for 9% of the time, Pallas kernels for 0%

commit v1 on v0

--- a/solution.py
+++ b/solution.py
@@ -9,6 +9,11 @@
 coef_linear = 3.4445
 coef_cubic = -4.775
 coef_quintic = 2.0315
+
+
+def gather_over(block, axis, d):
+    sent = jnp.stack([block] * lax.axis_size(axis))
+    return jnp.concatenate(lax.all_to_all(sent, axis, 0, 0), axis=d)
 
 
 def gathered_by_axis(shard, axes, dim):
@@ -99,10 +104,7 @@
     hid_width = fast_weights.shape[4]
     half_width = w_qkv.shape[3]
     projected = jnp.einsum(
-        "td,jde->jte",
-        tokens,
-        lax.all_gather(w_qkv[0], TOK, axis=1, tiled=True),
-        preferred_element_type=jnp.float32,
+        "td,jde->jte", tokens, gather_over(w_qkv[0], TOK, 1), preferred_element_type=jnp.float32
     )
     shaped = projected.reshape(3, tok_rows, local_heads, fan_width)
     queries = rms_rows(shaped[0], 1e-06).astype(jnp.bfloat16)

time: 376 us -> 581 us (1.55)
  waiting for transfers between devices: 286 us -> 452 us
  blocking collectives: 19.8 us -> 35.1 us
  local copies, waits for them, and re-layouts: 7.67 us -> 22 us
  starting transfers between devices: 1.39 us -> 13.8 us
    all_to_all x0 -> x1, waiting for transfers between devices: none -> 285 us  [gather_over(): return jnp.concatenate(lax.all_to_all(sent, axis, 0, 0), axis=d)]
    all_gather x1 -> x0, waiting for transfers between devices: 122 us -> none  [shards(): lax.all_gather(w_qkv[0], TOK, axis=1, tiled=True)]
    all_gather x1, blocking collectives: 10.9 us -> 26.2 us  [gathered_by_axis(): nearer = lax.all_gather(shard, axes[-1], axis=dim, tiled=True)]
    all_to_all x0 -> x1, starting transfers between devices: none -> 12.4 us  [gather_over(): return jnp.concatenate(lax.all_to_all(sent, axis, 0, 0), axis=d)]
    another operation x0 -> x1, local copies, waits for them, and re-layouts: none -> 7.08 us  [gather_over(): sent = jnp.stack([block] * lax.axis_size(axis))]
    all_to_all x0 -> x1, local copies, waits for them, and re-layouts: none -> 6.42 us  [gather_over(): return jnp.concatenate(lax.all_to_all(sent, axis, 0, 0), axis=d)]
  transfers between devices with their start and end apart: 4 -> 4, of which waited for: 3 -> 3; matrix products, arithmetic and copies ran while one was open for 9% -> 6% of each run, Pallas kernels for 0% -> 0%
where the time goes in v1:
time: 581 us; the launch traced here: 580 us
  waiting for transfers between devices  452 us (78%)
  blocking collectives  35.1 us (6%)
  matrix products  25.5 us (4%)
  local copies, waits for them, and re-layouts  22 us (4%)
  other arithmetic  16.4 us (3%)
  between operations  15.8 us (3%)
  starting transfers between devices  13.8 us (2%)
    all_to_all x1, waiting for transfers between devices, gather_over(): return jnp.concatenate(lax.all_to_all(sent, axis, 0, 0), axis=d)  285 us
    psum x1, waiting for transfers between devices, shards(): summed = lax.psum(gradients.astype(jnp.bfloat16), TOK).astype(jnp.float32)  162 us
    all_gather x1, blocking collectives, gathered_by_axis(): nearer = lax.all_gather(shard, axes[-1], axis=dim, tiled=True)  26.2 us
    all_to_all x1, starting transfers between devices, gather_over(): return jnp.concatenate(lax.all_to_all(sent, axis, 0, 0), axis=d)  12.4 us
  transfers between devices with their start and end apart: 4, of which 3 were waited for; matrix products, arithmetic and copies ran while one was open for 6% of the time, Pallas kernels for 0%

profile of v1, /device:TPU:1, one launch (start us, length us, event | category | flops | bytes accessed | tf_op | source)
XLA Modules:
  0.0 580.4 jit_solution(15801742802956196037)
XLA Ops:
  8.0 7.1 %stack.19 = bf16[32,3,64,1024]{3,2,1,0:T(8,128)(2,1)} broadcast(bf16[3,64,1024]{2,1,0:T(8,128)(2,1)} %bitcast.131), dimensions={1,2,3} | broadcast | bytes 12976128 | tf_op jit(solution)/shard_map/stack | solution.py:15
  15.1 12.4 %all-to-all-start = ((bf16[32,3,64,1024]{3,2,1,0:T(8,128)(2,1)}), bf16[32,3,64,1024]{3,2,1,0:T(8,128)(2,1)}, u32[]{:S(2)}, u32[]{:S(2)}) async-start(bf16[32,3,64,1024]{3,2,1,0:T(8,128)(2,1)} %stack.19), calls=%async_computation | async-start | bytes 25165824 | tf_op jit(solution)/shard_map/all_to_all | solution.py:16
  27.5 0.0 all-reduce.2.cloned.1.call-start
  27.5 0.0 copy-done.1
  27.5 1.9 copy.73
  29.4 285.1 %all-to-all-done = bf16[32,3,64,1024]{3,2,1,0:T(8,128)(2,1)} async-done(((bf16[32,3,64,1024]{3,2,1,0:T(8,128)(2,1)}), bf16[32,3,64,1024]{3,2,1,0:T(8,128)(2,1)}, u32[]{:S(2)}, u32[]{:S(2)}) %all-to-all-start) | async-done | bytes 12582944 | tf_op jit(solution)/shard_map/all_to_all | solution.py:16
  314.5 6.4 %copy.36 = bf16[32,3,64,1024]{3,2,0,1:T(8,128)(2,1)S(1)} copy(bf16[32,3,64,1024]{3,2,1,0:T(8,128)(2,1)} %all-to-all-done) | data formatting | bytes 25165824 | tf_op jit(solution)/shard_map/all_to_all | solution.py:16
  321.0 0.0 copy-done.9
  321.0 3.5 convolution_bitcast_fusion
  324.5 0.0 copy-start.3
  324.5 0.9 fusion.41
  325.4 0.1 multiply_reduce_fusion.3
  325.5 1.0 copy-done.3
  326.6 0.3 convolution_bitcast_fusion.4
  326.9 0.3 convolution_bitcast_fusion.5
  327.3 0.0 copy-done.13
  327.3 0.3 convolution_bitcast_fusion.6
  327.6 0.5 fusion.18
  328.1 0.5 fusion.17
  328.7 0.5 fusion.19
  329.1 0.0 copy-start.8
  329.2 2.0 pad_maximum_fusion
  331.2 0.0 all-reduce.2.cloned.1.call-update
  331.2 0.0 all-gather.4.cloned.1.call-start
  331.2 0.0 copy-done.8
  331.3 26.2 %all-gather = bf16[1,1024,256]{1,2,0:T(8,128)(2,1)} all-gather(bf16[1,1024,64]{1,2,0:T(8,128)(2,1)S(1)} %copy-done.8), channel_id=2, replica_groups=mesh['section'=4,'tok_0'=8,'tok_1'=4,'head'=2] {'tok_1'}, dimensions={2}, use_global_device_ids=true | all-gather | bytes 655360 | tf_op jit(solution)/shard_map/all_gather | solution.py:22
  357.4 0.0 all-gather.4.cloned.1.call-update
  357.5 1.1 multiply_reduce_fusion.2
  358.6 2.1 copy.45
  360.7 161.9 %all-reduce.2.cloned.1.call-done = bf16[2,3,512,512]{3,2,0,1:T(8,128)(2,1)} async-done(((bf16[2,3,512,512]{3,2,0,1:T(8,128)(2,1)}), bf16[2,3,512,512]{3,2,0,1:T(8,128)(2,1)}) %all-reduce.2.cloned.1.call-update) | async-done | bytes 3145744 | tf_op jit(solution)/shard_map/psum | solution.py:115
  522.6 3.5 multiply_reduce_fusion
  526.0 1.3 divide_convert_fusion
  527.3 0.2 copy.41
  527.6 1.8 convolution_convert_fusion.1
  529.4 1.8 fusion.42
  531.2 2.2 add_convert_fusion.1
  533.4 1.8 convolution_convert_fusion
  535.3 1.8 fusion.43
  537.1 0.0 copy-start.11
  537.1 2.5 fusion.5
  539.6 0.0 copy-start
  539.6 0.0 copy-done.11
  539.6 0.0 copy-start.7
  539.6 5.4 fusion.2
  545.0 0.0 copy-start.6
  545.0 1.7 copy-done.6
  546.7 1.1 convolution_bitcast_fusion.2
  547.8 2.6 multiply_reduce_fusion.1
  550.4 0.1 multiply_convert_fusion
  550.5 0.0 all-gather.4.cloned.1.call-done
  550.5 0.0 copy-start.10
  550.5 0.0 slice-start.1
  550.5 3.8 fusion.14
  554.4 0.0 copy-start.2
  554.4 8.9 %all_to_all.10 = bf16[2,128,1024]{2,1,0:T(8,128)(2,1)S(1)} all-to-all(bf16[2,128,1024]{2,1,0:T(8,128)(2,1)S(1)} %bitcast.127), channel_id=1, replica_groups=mesh['section'=4,'tok_0'=8,'tok_1'=4,'head'=2] {'head'}, dimensions={0} | all-to-all | bytes 1048576 | tf_op jit(solution)/shard_map/all_to_all | solution.py:34
  563.3 0.1 convert_reduce_fusion
  563.4 0.0 copy-done.10
  563.4 0.1 fusion.24
  563.5 1.3 collective-permute-start
  564.8 0.0 slice-done
  564.8 0.0 copy-done.2
  564.8 2.8 subtract_convert_fusion
  567.6 4.7 collective-permute-done
  572.3 0.7 copy.77
  (21 shorter events, 0.2 us)
Async XLA Ops:
  15.1 12.5 %copy-start.1 = (bf16[1,2,3,512,512]{4,3,2,1,0:T(8,128)(2,1)S(1)}, bf16[1,2,3,512,512]{4,3,2,1,0:T(8,128)(2,1)}, u32[]{:S(2)}) copy-start(bf16[1,2,3,512,512]{4,3,2,1,0:T(8,128)(2,1)} %param.12) | copy-start | bytes 9437188
  15.1 299.5 %all-to-all-start = ((bf16[32,3,64,1024]{3,2,1,0:T(8,128)(2,1)}), bf16[32,3,64,1024]{3,2,1,0:T(8,128)(2,1)}, u32[]{:S(2)}, u32[]{:S(2)}) async-start(bf16[32,3,64,1024]{3,2,1,0:T(8,128)(2,1)} %stack.19), calls=%async_computation | async-start | bytes 25165824 | tf_op jit(solution)/shard_map/all_to_all | solution.py:16
  27.5 495.1 %all-reduce.2.cloned.1.call-start = ((), (), s32[]{:S(2)}) async-start(), calls=%async_computation.2 | async-start | bytes 6291456 | tf_op jit(solution)/shard_map/psum | solution.py:115
  29.4 291.6 %copy-start.9 = (bf16[1,128,2048]{2,1,0:T(8,128)(2,1)S(1)}, bf16[1,128,2048]{2,1,0:T(8,128)(2,1)}, u32[]{:S(2)}) copy-start(bf16[1,128,2048]{2,1,0:T(8,128)(2,1)} %param.8) | copy-start | bytes 1572868
  324.5 2.1 copy-start.3
  325.4 1.9 copy-start.13
  329.1 2.1 copy-start.8
  331.2 191.4 %copy-start.4 = (bf16[1,2,3,512,512]{4,3,2,1,0:T(8,128)(2,1)S(1)}, bf16[1,2,3,512,512]{4,3,2,1,0:T(8,128)(2,1)}, u32[]{:S(2)}) copy-start(bf16[1,2,3,512,512]{4,3,2,1,0:T(8,128)(2,1)} %param.13) | copy-start | bytes 9437188
  331.2 191.4 %copy-start.12 = (f32[1,2]{1,0:T(1,128)S(1)}, f32[1,2]{1,0:T(1,128)}, u32[]{:S(2)}) copy-start(f32[1,2]{1,0:T(1,128)} %param.14) | copy-start | bytes 28
  331.2 219.3 %all-gather.4.cloned.1.call-start = ((), (), s32[]{:S(2)}) async-start(), calls=%async_computation.3 | async-start | bytes 4718592 | tf_op jit(solution)/shard_map/all_gather | solution.py:22
  522.6 3.5 copy-start.5
  537.1 2.5 copy-start.11
  539.6 5.4 copy-start
  539.6 7.1 %copy-start.7 = (f32[128,2,512]{2,0,1:T(8,128)S(1)}, f32[128,2,512]{2,0,1:T(8,128)}, u32[]{:S(2)}) copy-start(f32[128,2,512]{2,0,1:T(8,128)} %copy.45) | copy-start | bytes 1572868
  545.0 1.7 copy-start.6
  547.8 17.0 %slice-start = ((s8[6291456]{0:T(1024)(128)(4,1)}), s8[2097152]{0:T(1024)(128)(4,1)S(1)}, s32[]{:S(2)}) async-start(s8[6291456]{0:T(1024)(128)(4,1)} %bitcast.115), calls=%async_computation.4 | async-start | bytes 4194304
  550.5 12.9 %copy-start.10 = (bf16[1,128,2048]{2,1,0:T(8,128)(2,1)S(1)}, bf16[1,128,2048]{2,1,0:T(8,128)(2,1)}, u32[]{:S(2)}) copy-start(bf16[1,128,2048]{2,1,0:T(8,128)(2,1)} %param.8) | copy-start | bytes 1572868
  550.5 14.3 %slice-start.1 = ((s8[6291456]{0:T(1024)(128)(4,1)}), s8[4194304]{0:T(1024)(128)(4,1)S(1)}, s32[]{:S(2)}) async-start(s8[6291456]{0:T(1024)(128)(4,1)} %bitcast.115), calls=%async_computation.5 | async-start | bytes 8388608
  554.4 10.4 %copy-start.2 = (bf16[1,2,3,512,512]{4,3,2,1,0:T(8,128)(2,1)S(1)}, bf16[1,2,3,512,512]{4,3,2,1,0:T(8,128)(2,1)}, u32[]{:S(2)}) copy-start(bf16[1,2,3,512,512]{4,3,2,1,0:T(8,128)(2,1)} %param.12) | copy-start | bytes 9437188
  563.5 8.8 %collective-permute-start = (bf16[1,128,1024]{2,1,0:T(8,128)(2,1)S(1)}, bf16[1,128,1024]{2,1,0:T(8,128)(2,1)S(1)}, u32[]{:S(2)}, u32[]{:S(2)}) collective-permute-start(bf16[1,128,1024]{2,1,0:T(8,128)(2,1)S(1)} %fusion.24), channel_id=1, source_target_pairs={{0,64},{64,128},{128,192},{192,0},{1,65},{65,129},{129,193},{193,1... | collective-permute-start | bytes 786440 | tf_op jit(solution)/shard_map/ppermute | solution.py:41
Sparse Core Ops, SparseCore 0:
  331.3 191.1 all-reduce.1
Sparse Core Ops, SparseCore 1:
  357.6 68.1 all-gather.3
